TPU v7x, 32 devices: a whole 2x2x4 slice. The times are simulated.
32 devices in a mesh: slab: 8 (over z, x), blk: 4 (over y, core).
Axes of the slice: x: 2, y: 2, z: 4, core: 2. Of those that a mesh axis runs over, the one named last changes fastest.
Arguments:
- incident: float32 [16, 2, 336, 128], P('slab', None, 'blk'), may hold values from -6 to 6
- mie_coef: float32 [16, 2, 336], P('slab', None, 'blk'), may hold values from -0.6 to 0.6
- translation: bfloat16 [16, 8, 2, 336, 336], P('slab', None, None, 'blk'), may hold values from -0.078125 to 0.078125
- pair_shift: int32 [16, 8], P('slab'), may hold values from -1 to 1
- pair_member: int32 [16, 8], P('slab'), may hold values from 0 to 1
- positions: float32 [16, 3], P('slab'), may hold values from 0 to 1
- wave_index: int32 [256, 3], replicated, may hold values from -4 to 4
- plane_coef: bfloat16 [256, 2, 336], replicated, may hold values from -0.25 to 0.25
- ewald_weight: float32 [256], replicated, may hold values from 0.002 to 0.04
Outputs:
- basis_next: float32 [16, 2, 336, 128], P('slab', None, 'blk')
- residual: float32 [16, 2, 336, 128], P('slab', None, 'blk')
- hessenberg: float32 [9, 128], replicated
Inputs may be any that keep to these rules, and one draw needn't show every extreme that they name: `pair_shift`: each pair's source sphere lies in the target's slab or in one of the two slabs beside it on the periodic cycle of slabs.
All inputs are finite; a program needn't handle non-finite values.
Results may differ from a plain program's by a relative error of at most 0.004.
Values may be sent and summed in bfloat16 or wider, within the bound.
No kernel may reach another device: no remote copies, remote signals or barrier semaphores. Data moves between devices by JAX's collectives and lax.ppermute only.
A program may use at most 64 MiB of HBM per device.

v0:
```python
import jax
import jax.numpy as jnp
from jax import lax
from jax.sharding import PartitionSpec as P

two_pi = 6.283185307179586
epsilon = 1e-06
highest = lax.Precision.HIGHEST


def with_halo(cells, sides, width):
    for axis, dim in sides:
        count = lax.axis_size(axis)
        head = lax.slice_in_dim(cells, 0, width, axis=dim)
        tail = lax.slice_in_dim(cells, cells.shape[dim] - width, cells.shape[dim], axis=dim)
        cells = jnp.concatenate(
            [
                lax.ppermute(tail, axis, [(i, (i + 1) % count) for i in range(count)]),
                cells,
                lax.ppermute(head, axis, [((i + 1) % count, i) for i in range(count)]),
            ],
            axis=dim,
        )
    return cells


def complex_scale(coef_pair, basis):
    part_re = coef_pair[0] * basis[:, 0] - coef_pair[1] * basis[:, 1]
    part_im = coef_pair[0] * basis[:, 1] + coef_pair[1] * basis[:, 0]
    return jnp.stack([part_re, part_im], axis=1)


def inner_sum(left, right):
    part_re = jnp.sum(left[:, 0] * right[:, 0] + left[:, 1] * right[:, 1], axis=(0, 1))
    part_im = jnp.sum(left[:, 0] * right[:, 1] - left[:, 1] * right[:, 0], axis=(0, 1))
    return jnp.stack([part_re, part_im])


def plane_sums(projected, cos_part, sin_part):
    part_re = projected[:, 0, :, 0] - projected[:, 1, :, 1]
    part_im = projected[:, 0, :, 1] + projected[:, 1, :, 0]
    sum_re = jnp.sum(cos_part[:, :, None] * part_re + sin_part[:, :, None] * part_im, axis=1)
    sum_im = jnp.sum(cos_part[:, :, None] * part_im - sin_part[:, :, None] * part_re, axis=1)
    return jnp.stack([sum_re, sum_im], axis=1)


def plane_field(totals, coef_full, cos_part, sin_part, weights):
    total_re = totals[:, 0][:, None, :]
    total_im = totals[:, 1][:, None, :]
    turn_re = weights[:, None, None] * (
        cos_part[:, :, None] * total_re - sin_part[:, :, None] * total_im
    )
    turn_im = weights[:, None, None] * (
        cos_part[:, :, None] * total_im + sin_part[:, :, None] * total_re
    )
    turned = jnp.stack([turn_re, turn_im], axis=1)
    projected = jnp.einsum("gac,gbjn->jabcn", coef_full, turned, precision=highest)
    return jnp.stack(
        [projected[:, 0, 0] + projected[:, 1, 1], projected[:, 0, 1] - projected[:, 1, 0]], axis=1
    )


def apply_operator(
    vector, mie_coef, translation, source_rows, cos_part, sin_part, plane_coef, ewald_weight
):
    sphere_count = vector.shape[0]
    row_count = vector.shape[2]
    wave_count = plane_coef.shape[0]
    rounded = vector.astype(jnp.bfloat16)
    full_field = lax.all_gather(rounded, "blk", axis=2, tiled=True)
    extended = with_halo(full_field, (("slab", 0),), sphere_count)
    pair_count = translation.shape[0] * translation.shape[1]
    flat_trans = translation.reshape(pair_count, 2, row_count, translation.shape[4])
    sources = jnp.take(extended, source_rows, axis=0)
    product = jnp.einsum(
        "parc,pzcn->pazrn", flat_trans, sources, preferred_element_type=jnp.float32
    )
    near_re = product[:, 0, 0] - product[:, 1, 1]
    near_im = product[:, 0, 1] + product[:, 1, 0]
    near = (
        jnp.stack([near_re, near_im], axis=1)
        .reshape(sphere_count, translation.shape[1], 2, row_count, vector.shape[3])
        .sum(axis=1)
    )
    row_start = lax.axis_index("blk") * row_count
    coef_rows = lax.dynamic_slice_in_dim(plane_coef, row_start, row_count, 2)
    slice_count = wave_count // lax.axis_size("blk")
    wave_start = lax.axis_index("blk") * slice_count
    coef_slice = lax.dynamic_slice_in_dim(plane_coef, wave_start, slice_count, 0)
    cos_slice = lax.dynamic_slice_in_dim(cos_part, wave_start, slice_count, 0)
    sin_slice = lax.dynamic_slice_in_dim(sin_part, wave_start, slice_count, 0)
    projected = jnp.einsum(
        "gac,jbcn->gajbn", coef_slice, full_field, preferred_element_type=jnp.float32
    )
    partial_sums = plane_sums(projected, cos_slice, sin_slice)
    slice_total = lax.psum(partial_sums, "slab")
    totals = lax.all_gather(slice_total, "blk", axis=0, tiled=True)
    far = plane_field(totals, coef_rows.astype(jnp.float32), cos_part, sin_part, ewald_weight)
    summed = near + far
    scaled_re = (
        mie_coef[:, 0][:, :, None] * summed[:, 0] - mie_coef[:, 1][:, :, None] * summed[:, 1]
    )
    scaled_im = (
        mie_coef[:, 0][:, :, None] * summed[:, 1] + mie_coef[:, 1][:, :, None] * summed[:, 0]
    )
    return vector - jnp.stack([scaled_re, scaled_im], axis=1)


def squared(field):
    return jnp.sum(field * field, axis=(0, 1, 2))


def per_device(
    incident,
    mie_coef,
    translation,
    pair_shift,
    pair_member,
    positions,
    wave_index,
    plane_coef,
    ewald_weight,
):
    sphere_count = incident.shape[0]
    entries = sphere_count * lax.axis_size("slab") * incident.shape[2] * lax.axis_size("blk")
    source_rows = ((pair_shift + 1) * sphere_count + pair_member).reshape(-1)
    angles = two_pi * jnp.sum(
        wave_index.astype(jnp.float32)[:, None, :] * positions[None, :, :], axis=-1
    )
    cos_part = jnp.cos(angles)
    sin_part = jnp.sin(angles)

    def operator(vector):
        return apply_operator(
            vector, mie_coef, translation, source_rows, cos_part, sin_part, plane_coef, ewald_weight
        )

    start_total = lax.psum(squared(incident), ("slab", "blk"))
    beta = jnp.sqrt(start_total / entries + epsilon)
    first = incident / beta
    image = operator(first)
    proj_sum = lax.psum(inner_sum(first, image), ("slab", "blk"))
    h_one_one = proj_sum / entries
    image = image - complex_scale(h_one_one, first)
    first_total = lax.psum(squared(image), ("slab", "blk"))
    h_two_one = jnp.sqrt(first_total / entries + epsilon)
    basis_next = image / h_two_one
    image = operator(basis_next)
    h_one_two = lax.psum(inner_sum(first, image), ("slab", "blk")) / entries
    image = image - complex_scale(h_one_two, first)
    h_two_two = lax.psum(inner_sum(basis_next, image), ("slab", "blk")) / entries
    residual = image - complex_scale(h_two_two, basis_next)
    last_total = lax.psum(squared(residual), ("slab", "blk"))
    h_three_two = jnp.sqrt(last_total / entries + epsilon)
    hessenberg = jnp.stack(
        [
            beta,
            h_one_one[0],
            h_one_one[1],
            h_two_one,
            h_one_two[0],
            h_one_two[1],
            h_two_two[0],
            h_two_two[1],
            h_three_two,
        ]
    )
    return (basis_next, residual, hessenberg)


def solution(mesh):
    placed = (
        P("slab", None, "blk", None),
        P("slab", None, "blk"),
        P("slab", None, None, "blk", None),
        P("slab", None),
        P("slab", None),
        P("slab", None),
        P(),
        P(),
        P(),
    )
    return jax.shard_map(
        per_device,
        mesh=mesh,
        in_specs=placed,
        out_specs=(P("slab", None, "blk", None), P("slab", None, "blk", None), P()),
        check_vma=False,
    )
```

profile of v0, /device:TPU:0, one launch (start us, length us, event | category | flops | bytes accessed | tf_op | source)
XLA Modules:
  0.0 478.9 jit_solution(5836638708583548738)
XLA Ops:
  7.2 1.2 multiply_reduce_fusion.2
  8.5 42.0 %psum.56 = f32[128]{0:T(128)S(1)} all-reduce(f32[128]{0:T(128)S(1)} %multiply_reduce_fusion.2), channel_id=1, replica_groups=mesh['slab'=8,'blk'=4] {'slab','blk'}, use_global_device_ids=true, to_apply=%region_1.0 | all-reduce | flops 128 | bytes 1024 | tf_op jit(solution)/shard_map/psum | solution.py:138
  50.5 0.5 fusion.51
  51.0 0.9 copy_divide_fusion
  52.0 7.0 %all_gather.12 = bf16[2,2,336,128]{3,1,0,2:T(2,128)(2,1)S(1)} all-gather(bf16[2,2,84,128]{3,1,0,2:T(2,128)(2,1)S(1)} %copy.52), channel_id=1, replica_groups=mesh['slab'=8,'blk'=4] {'blk'}, dimensions={2}, use_global_device_ids=true | all-gather | bytes 430080 | tf_op jit(solution)/shard_map/all_gather | solution.py:70
  59.0 1.3 collective-permute-start
  60.3 3.4 collective-permute-start.1
  63.7 0.7 convert_element_type.12
  64.4 0.8 copy.55
  65.3 1.3 fusion.24
  66.8 0.6 pad_maximum_fusion.2
  67.5 0.7 multiply_add_fusion.5
  68.3 0.8 fusion.55
  69.1 65.3 %all-reduce.3.cloned.1.call-done = f32[64,2,128]{2,0,1:T(8,128)} async-done(((f32[64,2,128]{2,0,1:T(8,128)}), f32[64,2,128]{2,0,1:T(8,128)}) %all-reduce.3.cloned.1.call-update) | async-done | bytes 65552 | tf_op jit(solution)/shard_map/psum | solution.py:96
  134.3 6.0 %all_gather.13 = f32[256,2,128]{2,0,1:T(8,128)S(1)} all-gather(f32[64,2,128]{2,0,1:T(8,128)} %all-reduce.3.cloned.1.call-done), channel_id=1, replica_groups=mesh['slab'=8,'blk'=4] {'blk'}, dimensions={0}, use_global_device_ids=true | all-gather | bytes 327680 | tf_op jit(solution)/shard_map/all_gather | solution.py:97
  140.3 0.2 subtract_multiply_fusion.1
  140.6 1.3 convolution_bitcast_fusion.1
  141.9 0.7 copy-done.6
  142.7 2.5 pad_maximum_fusion
  145.2 8.9 %gather_fusion = bf16[16,2,336,128]{3,1,2,0:T(2,128)(2,1)} fusion(bf16[6,2,336,128]{3,1,0,2:T(2,128)(2,1)S(1)} %pad_maximum_fusion, s32[1024]{0:T(1024)S(1)} %pad_clamp_fusion), kind=kCustom, calls=%fused_computation.clone | custom fusion | bytes 5505088 | tf_op jit(solution)/shard_map/jit(_take)/gather | solution.py:74
  154.1 4.2 fusion.4
  158.3 0.9 fusion.8
  159.3 0.1 slice_subtract_fusion.1
  159.7 0.5 copy-done.1
  160.3 40.4 %psum.58 = f32[2,128]{1,0:T(2,128)S(1)} all-reduce(f32[2,128]{1,0:T(2,128)S(1)} %pad_maximum_fusion.4), channel_id=1, replica_groups=mesh['slab'=8,'blk'=4] {'slab','blk'}, use_global_device_ids=true, to_apply=%region_9.11 | all-reduce | flops 256 | bytes 2048 | tf_op jit(solution)/shard_map/psum | solution.py:142
  200.8 39.0 %psum.59 = f32[128]{0:T(128)S(1)} all-reduce(f32[128]{0:T(128)S(1)} %multiply_reduce_fusion.1), channel_id=1, replica_groups=mesh['slab'=8,'blk'=4] {'slab','blk'}, use_global_device_ids=true, to_apply=%region_11.13 | all-reduce | flops 128 | bytes 1024 | tf_op jit(solution)/shard_map/psum | solution.py:145
  239.8 0.5 fusion.52
  240.5 7.0 %all_gather.14 = bf16[2,2,336,128]{3,1,0,2:T(2,128)(2,1)S(1)} all-gather(bf16[2,2,84,128]{3,1,0,2:T(2,128)(2,1)S(1)} %copy.62), channel_id=1, replica_groups=mesh['slab'=8,'blk'=4] {'blk'}, dimensions={2}, use_global_device_ids=true | all-gather | bytes 430080 | tf_op jit(solution)/shard_map/all_gather | solution.py:70
  247.4 0.3 fusion.22
  247.9 0.6 pad_maximum_fusion.3
  248.5 1.4 collective-permute-start.2
  249.9 3.4 collective-permute-start.3
  253.3 0.8 copy.71
  254.1 70.2 %all-reduce.5.cloned.1.call-done = f32[64,2,128]{2,0,1:T(8,128)} async-done(((f32[64,2,128]{2,0,1:T(8,128)}), f32[64,2,128]{2,0,1:T(8,128)}) %all-reduce.5.cloned.1.call-update) | async-done | bytes 65552 | tf_op jit(solution)/shard_map/psum | solution.py:96
  324.3 6.0 %all_gather.15 = f32[256,2,128]{2,0,1:T(8,128)S(1)} all-gather(f32[64,2,128]{2,0,1:T(8,128)} %all-reduce.5.cloned.1.call-done), channel_id=1, replica_groups=mesh['slab'=8,'blk'=4] {'blk'}, dimensions={0}, use_global_device_ids=true | all-gather | bytes 327680 | tf_op jit(solution)/shard_map/all_gather | solution.py:97
  330.3 0.2 subtract_multiply_fusion
  330.5 0.4 convolution_bitcast_fusion
  330.9 0.7 fusion.32
  331.6 2.6 pad_maximum_fusion.1
  334.2 9.0 %gather_fusion.1 = bf16[16,2,336,128]{3,1,2,0:T(2,128)(2,1)} fusion(bf16[6,2,336,128]{3,1,0,2:T(2,128)(2,1)S(1)} %pad_maximum_fusion.1, s32[1024]{0:T(1024)} %copy-done.9), kind=kCustom, calls=%fused_computation.1.clone | custom fusion | bytes 5505088 | tf_op jit(solution)/shard_map/jit(_take)/gather | solution.py:74
  343.1 4.2 fusion.5
  347.4 0.9 fusion.13
  348.6 0.6 copy-done.5
  349.4 40.4 %psum.61 = f32[2,128]{1,0:T(2,128)S(1)} all-reduce(f32[2,128]{1,0:T(2,128)S(1)} %pad_maximum_fusion.5), channel_id=1, replica_groups=mesh['slab'=8,'blk'=4] {'slab','blk'}, use_global_device_ids=true, to_apply=%region_18.20 | all-reduce | flops 256 | bytes 2048 | tf_op jit(solution)/shard_map/psum | solution.py:149
  390.0 39.1 %psum.62 = f32[2,128]{1,0:T(2,128)S(1)} all-reduce(f32[2,128]{1,0:T(2,128)S(1)} %pad_maximum_fusion.6), channel_id=1, replica_groups=mesh['slab'=8,'blk'=4] {'slab','blk'}, use_global_device_ids=true, to_apply=%region_21.23 | all-reduce | flops 256 | bytes 2048 | tf_op jit(solution)/shard_map/psum | solution.py:151
  429.2 40.9 %psum.63 = f32[128]{0:T(128)S(1)} all-reduce(f32[128]{0:T(128)S(1)} %get-tuple-element.23), channel_id=1, replica_groups=mesh['slab'=8,'blk'=4] {'slab','blk'}, use_global_device_ids=true, to_apply=%region_23.25 | all-reduce | flops 128 | bytes 1024 | tf_op jit(solution)/shard_map/psum | solution.py:153
  470.0 0.8 copy.72
  470.8 1.2 stack.142
  (77 shorter events, 2.1 us)
Async XLA Ops:
  7.2 151.1 %copy-start = (bf16[2,8,2,84,336]{4,2,3,1,0:T(2,128)(2,1)S(1)}, bf16[2,8,2,84,336]{4,2,3,1,0:T(2,128)(2,1)}, u32[]{:S(2)}) copy-start(bf16[2,8,2,84,336]{4,2,3,1,0:T(2,128)(2,1)} %param.13) | copy-start | bytes 5419012
  7.2 133.1 %copy-start.10 = (f32[256]{0:T(256)S(1)}, f32[256]{0:T(256)}, u32[]{:S(2)}) copy-start(f32[256]{0:T(256)} %param.19) | copy-start | bytes 3076
  7.2 127.1 %all-reduce.3.cloned.1.call-start = ((), (), s32[]{:S(2)}) async-start(), calls=%async_computation | async-start | bytes 131072 | tf_op jit(solution)/shard_map/psum | solution.py:96
  59.0 82.9 %copy-start.2 = (bf16[2,2,336,128]{3,1,0,2:T(2,128)(2,1)}, bf16[2,2,336,128]{3,1,0,2:T(2,128)(2,1)S(1)}, u32[]{:S(2)}) copy-start(bf16[2,2,336,128]{3,1,0,2:T(2,128)(2,1)S(1)} %all_gather.12) | copy-start | bytes 1032196
  59.0 82.9 %collective-permute-start = (bf16[2,2,336,128]{3,1,0,2:T(2,128)(2,1)S(1)}, bf16[2,2,336,128]{3,1,0,2:T(2,128)(2,1)S(1)}, u32[]{:S(2)}, u32[]{:S(2)}) collective-permute-start(bf16[2,2,336,128]{3,1,0,2:T(2,128)(2,1)S(1)} %all_gather.12), channel_id=1, source_target_pairs={{0,4},{4,8},{8,12},{12,16},{16,20},{20,24},{24,28},{28,0},{1,5},{5... | collective-permute-start | bytes 1032200 | tf_op jit(solution)/shard_map/ppermute | solution.py:18
  60.3 82.4 %collective-permute-start.1 = (bf16[2,2,336,128]{3,1,0,2:T(2,128)(2,1)S(1)}, bf16[2,2,336,128]{3,1,0,2:T(2,128)(2,1)}, u32[]{:S(2)}, u32[]{:S(2)}) collective-permute-start(bf16[2,2,336,128]{3,1,0,2:T(2,128)(2,1)S(1)} %all_gather.12), channel_id=1, source_target_pairs={{4,0},{8,4},{12,8},{16,12},{20,16},{24,20},{28,24},{0,28},{5,1},{9... | collective-permute-start | bytes 1032200 | tf_op jit(solution)/shard_map/ppermute | solution.py:20
  67.4 256.9 %all-reduce.5.cloned.1.call-start = ((), (), s32[]{:S(2)}) async-start(), calls=%async_computation.1 | async-start | bytes 131072 | tf_op jit(solution)/shard_map/psum | solution.py:96
  68.3 85.8 %copy-start.11 = (pred[16]{0:T(512)(128)(4,1)}, pred[16]{0:T(512)(128)(4,1)S(1)}, u32[]{:S(2)}) copy-start(pred[16]{0:T(512)(128)(4,1)S(1)} %compare_and_fusion) | copy-start | bytes 52
  69.1 85.0 %copy-start.9 = (s32[1024]{0:T(1024)}, s32[1024]{0:T(1024)S(1)}, u32[]{:S(2)}) copy-start(s32[1024]{0:T(1024)S(1)} %pad_clamp_fusion) | copy-start | bytes 12292
  141.9 0.7 copy-start.6
  159.2 0.9 copy-start.1
  159.4 88.0 %copy-start.4 = (bf16[256,2,336]{0,2,1:T(8,128)(2,1)S(1)}, bf16[256,2,336]{0,2,1:T(8,128)(2,1)}, u32[]{:S(2)}) copy-start(bf16[256,2,336]{0,2,1:T(8,128)(2,1)} %param.18) | copy-start | bytes 1032196
  200.6 129.9 %copy-start.7 = (f32[2,128]{1,0:T(2,128)}, f32[2,128]{1,0:T(2,128)S(1)}, u32[]{:S(2)}) copy-start(f32[2,128]{1,0:T(2,128)S(1)} %broadcast_multiply_fusion.2) | copy-start | bytes 3076
  247.4 84.2 %copy-start.3 = (bf16[2,2,336,128]{3,1,0,2:T(2,128)(2,1)}, bf16[2,2,336,128]{3,1,0,2:T(2,128)(2,1)S(1)}, u32[]{:S(2)}) copy-start(bf16[2,2,336,128]{3,1,0,2:T(2,128)(2,1)S(1)} %all_gather.14) | copy-start | bytes 1032196
  248.5 83.1 %collective-permute-start.2 = (bf16[2,2,336,128]{3,1,0,2:T(2,128)(2,1)S(1)}, bf16[2,2,336,128]{3,1,0,2:T(2,128)(2,1)}, u32[]{:S(2)}, u32[]{:S(2)}) collective-permute-start(bf16[2,2,336,128]{3,1,0,2:T(2,128)(2,1)S(1)} %all_gather.14), channel_id=1, source_target_pairs={{0,4},{4,8},{8,12},{12,16},{16,20},{20,24},{24,28},{28,0},{1,5},{5... | collective-permute-start | bytes 1032200 | tf_op jit(solution)/shard_map/ppermute | solution.py:18
  249.9 81.7 %collective-permute-start.3 = (bf16[2,2,336,128]{3,1,0,2:T(2,128)(2,1)S(1)}, bf16[2,2,336,128]{3,1,0,2:T(2,128)(2,1)}, u32[]{:S(2)}, u32[]{:S(2)}) collective-permute-start(bf16[2,2,336,128]{3,1,0,2:T(2,128)(2,1)S(1)} %all_gather.14), channel_id=1, source_target_pairs={{4,0},{8,4},{12,8},{16,12},{20,16},{24,20},{28,24},{0,28},{5,1},{9... | collective-permute-start | bytes 1032200 | tf_op jit(solution)/shard_map/ppermute | solution.py:20
  348.3 0.9 copy-start.5
  348.5 122.2 %copy-start.8 = (f32[2,128]{1,0:T(2,128)S(1)}, f32[2,128]{1,0:T(2,128)}, u32[]{:S(2)}) copy-start(f32[2,128]{1,0:T(2,128)} %copy-done.7) | copy-start | bytes 3076
  348.6 122.2 %copy-start.12 = (f32[1,128]{1,0:T(1,128)S(1)}, f32[1,128]{1,0:T(1,128)}, u32[]{:S(2)}) copy-start(f32[1,128]{1,0:T(1,128)} %get-tuple-element.65) | copy-start | bytes 1540
  348.6 122.2 %copy-start.13 = (f32[1,128]{1,0:T(1,128)S(1)}, f32[1,128]{1,0:T(1,128)}, u32[]{:S(2)}) copy-start(f32[1,128]{1,0:T(1,128)} %get-tuple-element.63) | copy-start | bytes 1540
Sparse Core Ops, SparseCore 0:
  67.5 66.7 all-reduce.2
  248.7 75.5 all-reduce.4
where the time goes:
time: 480 us; the launch traced here: 479 us
  blocking collectives  268 us (56%)
  waiting for transfers between devices  136 us (28%)
  local copies, waits for them, and re-layouts  24.4 us (5%)
  other arithmetic  22.3 us (5%)
  between operations  14.4 us (3%)
  starting transfers between devices  9.58 us (2%)
  matrix products  5.11 us (1%)
    psum x2, waiting for transfers between devices, apply_operator(): slice_total = lax.psum(partial_sums, 'slab')  135 us
    psum x1, blocking collectives, per_device(): start_total = lax.psum(squared(incident), ('slab', 'blk'))  42 us
    psum x1, blocking collectives, per_device(): last_total = lax.psum(squared(residual), ('slab', 'blk'))  40.9 us
    psum x1, blocking collectives, per_device(): h_one_two = lax.psum(inner_sum(first, image), ('slab', 'blk')) / entries  40.4 us
    psum x1, blocking collectives, per_device(): proj_sum = lax.psum(inner_sum(first, image), ('slab', 'blk'))  40.4 us
    psum x1, blocking collectives, per_device(): lax.psum(inner_sum(basis_next, image), ('slab', 'blk')) / entries  39.1 us
    psum x1, blocking collectives, per_device(): first_total = lax.psum(squared(image), ('slab', 'blk'))  39 us
    gather x2, local copies, waits for them, and re-layouts, apply_operator(): sources = jnp.take(extended, source_rows, axis=0)  17.8 us
  transfers between devices with their start and end apart: 6, of which 2 were waited for; matrix products, arithmetic and copies ran while one was open for 2% of the time, Pallas kernels for 0%

commit v1 on v0

--- a/solution.py
+++ b/solution.py
@@ -150,7 +150,13 @@
     image = image - complex_scale(h_one_two, first)
     h_two_two = lax.psum(inner_sum(basis_next, image), ("slab", "blk")) / entries
     residual = image - complex_scale(h_two_two, basis_next)
-    last_total = lax.psum(squared(residual), ("slab", "blk"))
+
+    def _report_lane(own_rows):
+        for ii in ("blk", "slab"):
+            own_rows = jax.lax.psum(own_rows, ii)
+        return own_rows
+
+    last_total = _report_lane(squared(residual))
     h_three_two = jnp.sqrt(last_total / entries + epsilon)
     hessenberg = jnp.stack(
         [

time: 480 us -> 466 us (0.971)
  blocking collectives: 268 us -> 253 us
    psum x1 -> x2, blocking collectives: 40.9 us -> 26.7 us  [_report_lane(): own_rows = jax.lax.psum(own_rows, ii)]
where the time goes in v1:
time: 466 us; the launch traced here: 465 us
  blocking collectives  253 us (54%)
  waiting for transfers between devices  136 us (29%)
  local copies, waits for them, and re-layouts  24.4 us (5%)
  other arithmetic  22.3 us (5%)
  between operations  14.4 us (3%)
  starting transfers between devices  9.58 us (2%)
  matrix products  5.11 us (1%)
    psum x2, waiting for transfers between devices, apply_operator(): slice_total = lax.psum(partial_sums, 'slab')  135 us
    psum x1, blocking collectives, per_device(): start_total = lax.psum(squared(incident), ('slab', 'blk'))  42 us
    psum x1, blocking collectives, per_device(): proj_sum = lax.psum(inner_sum(first, image), ('slab', 'blk'))  40.4 us
    psum x1, blocking collectives, per_device(): h_one_two = lax.psum(inner_sum(first, image), ('slab', 'blk')) / entries  40.2 us
    psum x1, blocking collectives, per_device(): lax.psum(inner_sum(basis_next, image), ('slab', 'blk')) / entries  39.1 us
    psum x1, blocking collectives, per_device(): first_total = lax.psum(squared(image), ('slab', 'blk'))  39 us
    psum x2, blocking collectives, _report_lane(): own_rows = jax.lax.psum(own_rows, ii)  26.7 us
    gather x2, local copies, waits for them, and re-layouts, apply_operator(): sources = jnp.take(extended, source_rows, axis=0)  17.8 us
  transfers between devices with their start and end apart: 6, of which 2 were waited for; matrix products, arithmetic and copies ran while one was open for 2% of the time, Pallas kernels for 0%

profile of v1, /device:TPU:0, one launch (start us, length us, event | category | flops | bytes accessed | tf_op | source)
XLA Modules:
  0.0 464.5 jit_solution(5032423188420116818)
XLA Ops:
  7.2 1.2 multiply_reduce_fusion.2
  8.5 42.0 %psum.63 = f32[128]{0:T(128)S(1)} all-reduce(f32[128]{0:T(128)S(1)} %multiply_reduce_fusion.2), channel_id=1, replica_groups=mesh['slab'=8,'blk'=4] {'slab','blk'}, use_global_device_ids=true, to_apply=%region_1.0 | all-reduce | flops 128 | bytes 1024 | tf_op jit(solution)/shard_map/psum | solution.py:138
  50.5 0.5 fusion.51
  51.0 0.9 copy_divide_fusion
  52.0 7.0 %all_gather.12 = bf16[2,2,336,128]{3,1,0,2:T(2,128)(2,1)S(1)} all-gather(bf16[2,2,84,128]{3,1,0,2:T(2,128)(2,1)S(1)} %copy.52), channel_id=1, replica_groups=mesh['slab'=8,'blk'=4] {'blk'}, dimensions={2}, use_global_device_ids=true | all-gather | bytes 430080 | tf_op jit(solution)/shard_map/all_gather | solution.py:70
  59.0 1.3 collective-permute-start
  60.3 3.4 collective-permute-start.1
  63.7 0.7 convert_element_type.12
  64.4 0.8 copy.55
  65.3 1.3 fusion.24
  66.8 0.6 pad_maximum_fusion.2
  67.5 0.7 multiply_add_fusion.5
  68.3 0.8 fusion.55
  69.1 65.3 %all-reduce.3.cloned.1.call-done = f32[64,2,128]{2,0,1:T(8,128)} async-done(((f32[64,2,128]{2,0,1:T(8,128)}), f32[64,2,128]{2,0,1:T(8,128)}) %all-reduce.3.cloned.1.call-update) | async-done | bytes 65552 | tf_op jit(solution)/shard_map/psum | solution.py:96
  134.3 6.0 %all_gather.13 = f32[256,2,128]{2,0,1:T(8,128)S(1)} all-gather(f32[64,2,128]{2,0,1:T(8,128)} %all-reduce.3.cloned.1.call-done), channel_id=1, replica_groups=mesh['slab'=8,'blk'=4] {'blk'}, dimensions={0}, use_global_device_ids=true | all-gather | bytes 327680 | tf_op jit(solution)/shard_map/all_gather | solution.py:97
  140.3 0.2 subtract_multiply_fusion.1
  140.6 1.3 convolution_bitcast_fusion.1
  141.9 0.7 copy-done.6
  142.7 2.5 pad_maximum_fusion
  145.2 8.9 %gather_fusion = bf16[16,2,336,128]{3,1,2,0:T(2,128)(2,1)} fusion(bf16[6,2,336,128]{3,1,0,2:T(2,128)(2,1)S(1)} %pad_maximum_fusion, s32[1024]{0:T(1024)S(1)} %pad_clamp_fusion), kind=kCustom, calls=%fused_computation.clone | custom fusion | bytes 5505088 | tf_op jit(solution)/shard_map/jit(_take)/gather | solution.py:74
  154.1 4.2 fusion.4
  158.3 0.9 fusion.8
  159.7 0.5 copy-done.1
  160.3 40.4 %psum.65 = f32[2,128]{1,0:T(2,128)S(1)} all-reduce(f32[2,128]{1,0:T(2,128)S(1)} %pad_maximum_fusion.4), channel_id=1, replica_groups=mesh['slab'=8,'blk'=4] {'slab','blk'}, use_global_device_ids=true, to_apply=%region_9.11 | all-reduce | flops 256 | bytes 2048 | tf_op jit(solution)/shard_map/psum | solution.py:142
  200.8 39.0 %psum.66 = f32[128]{0:T(128)S(1)} all-reduce(f32[128]{0:T(128)S(1)} %multiply_reduce_fusion.1), channel_id=1, replica_groups=mesh['slab'=8,'blk'=4] {'slab','blk'}, use_global_device_ids=true, to_apply=%region_11.13 | all-reduce | flops 128 | bytes 1024 | tf_op jit(solution)/shard_map/psum | solution.py:145
  239.8 0.5 fusion.52
  240.5 7.0 %all_gather.14 = bf16[2,2,336,128]{3,1,0,2:T(2,128)(2,1)S(1)} all-gather(bf16[2,2,84,128]{3,1,0,2:T(2,128)(2,1)S(1)} %copy.62), channel_id=1, replica_groups=mesh['slab'=8,'blk'=4] {'blk'}, dimensions={2}, use_global_device_ids=true | all-gather | bytes 430080 | tf_op jit(solution)/shard_map/all_gather | solution.py:70
  247.4 0.3 fusion.22
  247.9 0.6 pad_maximum_fusion.3
  248.5 1.4 collective-permute-start.2
  249.9 3.4 collective-permute-start.3
  253.3 0.8 copy.71
  254.1 70.2 %all-reduce.5.cloned.1.call-done = f32[64,2,128]{2,0,1:T(8,128)} async-done(((f32[64,2,128]{2,0,1:T(8,128)}), f32[64,2,128]{2,0,1:T(8,128)}) %all-reduce.5.cloned.1.call-update) | async-done | bytes 65552 | tf_op jit(solution)/shard_map/psum | solution.py:96
  324.3 6.0 %all_gather.15 = f32[256,2,128]{2,0,1:T(8,128)S(1)} all-gather(f32[64,2,128]{2,0,1:T(8,128)} %all-reduce.5.cloned.1.call-done), channel_id=1, replica_groups=mesh['slab'=8,'blk'=4] {'blk'}, dimensions={0}, use_global_device_ids=true | all-gather | bytes 327680 | tf_op jit(solution)/shard_map/all_gather | solution.py:97
  330.3 0.2 subtract_multiply_fusion
  330.5 0.4 convolution_bitcast_fusion
  330.9 0.7 fusion.32
  331.6 2.6 pad_maximum_fusion.1
  334.2 9.0 %gather_fusion.1 = bf16[16,2,336,128]{3,1,2,0:T(2,128)(2,1)} fusion(bf16[6,2,336,128]{3,1,0,2:T(2,128)(2,1)S(1)} %pad_maximum_fusion.1, s32[1024]{0:T(1024)} %copy-done.9), kind=kCustom, calls=%fused_computation.1.clone | custom fusion | bytes 5505088 | tf_op jit(solution)/shard_map/jit(_take)/gather | solution.py:74
  343.1 4.2 fusion.5
  347.4 0.9 fusion.13
  348.6 0.6 copy-done.5
  349.4 40.2 %psum.68 = f32[2,128]{1,0:T(2,128)S(1)} all-reduce(f32[2,128]{1,0:T(2,128)S(1)} %pad_maximum_fusion.5), channel_id=1, replica_groups=mesh['slab'=8,'blk'=4] {'slab','blk'}, use_global_device_ids=true, to_apply=%region_18.20 | all-reduce | flops 256 | bytes 2048 | tf_op jit(solution)/shard_map/psum | solution.py:149
  389.8 39.1 %psum.69 = f32[2,128]{1,0:T(2,128)S(1)} all-reduce(f32[2,128]{1,0:T(2,128)S(1)} %pad_maximum_fusion.6), channel_id=1, replica_groups=mesh['slab'=8,'blk'=4] {'slab','blk'}, use_global_device_ids=true, to_apply=%region_21.23 | all-reduce | flops 256 | bytes 2048 | tf_op jit(solution)/shard_map/psum | solution.py:151
  428.9 6.3 %psum.70 = f32[128]{0:T(128)S(1)} all-reduce(f32[128]{0:T(128)S(1)} %get-tuple-element.23), channel_id=1, replica_groups=mesh['slab'=8,'blk'=4] {'blk'}, use_global_device_ids=true, to_apply=%region_23.25 | all-reduce | flops 128 | bytes 1024 | tf_op jit(solution)/shard_map/psum | solution.py:156
  435.2 20.4 %psum.71 = f32[128]{0:T(128)S(1)} all-reduce(f32[128]{0:T(128)S(1)} %psum.70), channel_id=1, replica_groups=mesh['slab'=8,'blk'=4] {'slab'}, use_global_device_ids=true, to_apply=%region_24.26 | all-reduce | flops 128 | bytes 1024 | tf_op jit(solution)/shard_map/psum | solution.py:156
  455.7 0.8 copy.72
  456.5 1.2 stack.142
  (78 shorter events, 2.2 us)
Async XLA Ops:
  7.2 151.1 %copy-start = (bf16[2,8,2,84,336]{4,2,3,1,0:T(2,128)(2,1)S(1)}, bf16[2,8,2,84,336]{4,2,3,1,0:T(2,128)(2,1)}, u32[]{:S(2)}) copy-start(bf16[2,8,2,84,336]{4,2,3,1,0:T(2,128)(2,1)} %param.13) | copy-start | bytes 5419012
  7.2 133.1 %copy-start.10 = (f32[256]{0:T(256)S(1)}, f32[256]{0:T(256)}, u32[]{:S(2)}) copy-start(f32[256]{0:T(256)} %param.19) | copy-start | bytes 3076
  7.2 127.1 %all-reduce.3.cloned.1.call-start = ((), (), s32[]{:S(2)}) async-start(), calls=%async_computation | async-start | bytes 131072 | tf_op jit(solution)/shard_map/psum | solution.py:96
  59.0 82.9 %copy-start.2 = (bf16[2,2,336,128]{3,1,0,2:T(2,128)(2,1)}, bf16[2,2,336,128]{3,1,0,2:T(2,128)(2,1)S(1)}, u32[]{:S(2)}) copy-start(bf16[2,2,336,128]{3,1,0,2:T(2,128)(2,1)S(1)} %all_gather.12) | copy-start | bytes 1032196
  59.0 82.9 %collective-permute-start = (bf16[2,2,336,128]{3,1,0,2:T(2,128)(2,1)S(1)}, bf16[2,2,336,128]{3,1,0,2:T(2,128)(2,1)S(1)}, u32[]{:S(2)}, u32[]{:S(2)}) collective-permute-start(bf16[2,2,336,128]{3,1,0,2:T(2,128)(2,1)S(1)} %all_gather.12), channel_id=1, source_target_pairs={{0,4},{4,8},{8,12},{12,16},{16,20},{20,24},{24,28},{28,0},{1,5},{5... | collective-permute-start | bytes 1032200 | tf_op jit(solution)/shard_map/ppermute | solution.py:18
  60.3 82.4 %collective-permute-start.1 = (bf16[2,2,336,128]{3,1,0,2:T(2,128)(2,1)S(1)}, bf16[2,2,336,128]{3,1,0,2:T(2,128)(2,1)}, u32[]{:S(2)}, u32[]{:S(2)}) collective-permute-start(bf16[2,2,336,128]{3,1,0,2:T(2,128)(2,1)S(1)} %all_gather.12), channel_id=1, source_target_pairs={{4,0},{8,4},{12,8},{16,12},{20,16},{24,20},{28,24},{0,28},{5,1},{9... | collective-permute-start | bytes 1032200 | tf_op jit(solution)/shard_map/ppermute | solution.py:20
  67.4 256.9 %all-reduce.5.cloned.1.call-start = ((), (), s32[]{:S(2)}) async-start(), calls=%async_computation.1 | async-start | bytes 131072 | tf_op jit(solution)/shard_map/psum | solution.py:96
  68.3 85.8 %copy-start.11 = (pred[16]{0:T(512)(128)(4,1)}, pred[16]{0:T(512)(128)(4,1)S(1)}, u32[]{:S(2)}) copy-start(pred[16]{0:T(512)(128)(4,1)S(1)} %compare_and_fusion) | copy-start | bytes 52
  69.1 85.0 %copy-start.9 = (s32[1024]{0:T(1024)}, s32[1024]{0:T(1024)S(1)}, u32[]{:S(2)}) copy-start(s32[1024]{0:T(1024)S(1)} %pad_clamp_fusion) | copy-start | bytes 12292
  141.9 0.7 copy-start.6
  159.2 0.9 copy-start.1
  159.4 88.0 %copy-start.4 = (bf16[256,2,336]{0,2,1:T(8,128)(2,1)S(1)}, bf16[256,2,336]{0,2,1:T(8,128)(2,1)}, u32[]{:S(2)}) copy-start(bf16[256,2,336]{0,2,1:T(8,128)(2,1)} %param.18) | copy-start | bytes 1032196
  200.6 129.9 %copy-start.7 = (f32[2,128]{1,0:T(2,128)}, f32[2,128]{1,0:T(2,128)S(1)}, u32[]{:S(2)}) copy-start(f32[2,128]{1,0:T(2,128)S(1)} %broadcast_multiply_fusion.2) | copy-start | bytes 3076
  247.4 84.2 %copy-start.3 = (bf16[2,2,336,128]{3,1,0,2:T(2,128)(2,1)}, bf16[2,2,336,128]{3,1,0,2:T(2,128)(2,1)S(1)}, u32[]{:S(2)}) copy-start(bf16[2,2,336,128]{3,1,0,2:T(2,128)(2,1)S(1)} %all_gather.14) | copy-start | bytes 1032196
  248.5 83.1 %collective-permute-start.2 = (bf16[2,2,336,128]{3,1,0,2:T(2,128)(2,1)S(1)}, bf16[2,2,336,128]{3,1,0,2:T(2,128)(2,1)}, u32[]{:S(2)}, u32[]{:S(2)}) collective-permute-start(bf16[2,2,336,128]{3,1,0,2:T(2,128)(2,1)S(1)} %all_gather.14), channel_id=1, source_target_pairs={{0,4},{4,8},{8,12},{12,16},{16,20},{20,24},{24,28},{28,0},{1,5},{5... | collective-permute-start | bytes 1032200 | tf_op jit(solution)/shard_map/ppermute | solution.py:18
  249.9 81.7 %collective-permute-start.3 = (bf16[2,2,336,128]{3,1,0,2:T(2,128)(2,1)S(1)}, bf16[2,2,336,128]{3,1,0,2:T(2,128)(2,1)}, u32[]{:S(2)}, u32[]{:S(2)}) collective-permute-start(bf16[2,2,336,128]{3,1,0,2:T(2,128)(2,1)S(1)} %all_gather.14), channel_id=1, source_target_pairs={{4,0},{8,4},{12,8},{16,12},{20,16},{24,20},{28,24},{0,28},{5,1},{9... | collective-permute-start | bytes 1032200 | tf_op jit(solution)/shard_map/ppermute | solution.py:20
  348.3 0.9 copy-start.5
  348.5 107.9 %copy-start.8 = (f32[2,128]{1,0:T(2,128)S(1)}, f32[2,128]{1,0:T(2,128)}, u32[]{:S(2)}) copy-start(f32[2,128]{1,0:T(2,128)} %copy-done.7) | copy-start | bytes 3076
  348.6 107.9 %copy-start.12 = (f32[1,128]{1,0:T(1,128)S(1)}, f32[1,128]{1,0:T(1,128)}, u32[]{:S(2)}) copy-start(f32[1,128]{1,0:T(1,128)} %get-tuple-element.65) | copy-start | bytes 1540
  348.6 107.9 %copy-start.13 = (f32[1,128]{1,0:T(1,128)S(1)}, f32[1,128]{1,0:T(1,128)}, u32[]{:S(2)}) copy-start(f32[1,128]{1,0:T(1,128)} %get-tuple-element.63) | copy-start | bytes 1540
Sparse Core Ops, SparseCore 0:
  67.5 66.7 all-reduce.2
  248.7 75.5 all-reduce.4
